TPU v7x, 32 devices: a whole 2x2x4 slice. The times are simulated.
32 devices in a mesh: comp: 2 (over x), rows: 4 (over z), cols: 4 (over y, core).
Axes of the slice: x: 2, y: 2, z: 4, core: 2. Of those that a mesh axis runs over, the one named last changes fastest.
Arguments:
- atm_state: float32 [4, 4, 256, 512], P(None, None, ('comp', 'rows'), 'cols'), may hold values from -6 to 6
- ocean_state: float32 [4, 8, 128, 512], P(None, None, ('comp', 'rows'), 'cols'), may hold values from -6 to 6
- coupling: float32 [256, 512], P(('comp', 'rows'), 'cols'), may hold values from 0.2 to 2
- down_weights: bfloat16 [8, 128, 128, 128], P(('comp', 'rows'), 'cols'), may hold values from -0.5 to 0.5
- down_src: int32 [8, 128], P(('comp', 'rows'), 'cols'), may hold values from 0 to 31
- down_row: int32 [8, 128], P(('comp', 'rows'), 'cols'), may hold values from 0 to 3, as said below
- down_blk: int32 [8, 128], P(('comp', 'rows'), 'cols'), may hold values from 0 to 15
- up_weights: bfloat16 [8, 128, 128, 128], P(('comp', 'rows'), 'cols'), may hold values from -0.5 to 0.5
- up_dst: int32 [8, 128], P(('comp', 'rows'), 'cols'), may hold values from 0 to 31
- up_src: int32 [8, 128], P(('comp', 'rows'), 'cols'), may hold values from 0 to 63, as said below
Outputs:
- atm_out: float32 [4, 4, 256, 512], P(None, None, ('comp', 'rows'), 'cols')
- ocean_out: float32 [4, 8, 128, 512], P(None, None, ('comp', 'rows'), 'cols')
Inputs may be any that keep to these rules, and one draw needn't show every extreme that they name: `down_row`: among one device's 32 down entries, no rows index is named more than 16 times, and some rows index exactly 16 times. `up_src`: no two of one device's 32 up entries name the same value; at most 16 of them come from one rows index, and exactly 16 from some rows index.
All inputs are finite; a program needn't handle non-finite values.
Results may differ from a plain program's by a relative error of at most 0.0003.
Values sent between devices are 32-bit elements; how exact they have to be, the bound alone decides.
A program may use at most 64 MiB of HBM per device.

v0:
```python
import jax
import jax.numpy as jnp
import numpy as np
from jax import lax
from jax.sharding import PartitionSpec as P

NP = 4


EXACT = lax.Precision.HIGHEST
VISCOSITY = 0.01
ATM_GAIN = 0.5
DIFFUSION = 0.1
SEA_GAIN = 0.5


def with_halo(cells, sides, width, closed):
    for axis, dim in sides:
        count = lax.axis_size(axis)
        ends = count if closed else count - 1
        head = lax.slice_in_dim(cells, 0, width, axis=dim)
        tail = lax.slice_in_dim(cells, cells.shape[dim] - width, cells.shape[dim], axis=dim)
        cells = jnp.concatenate(
            [
                lax.ppermute(tail, axis, [(i, (i + 1) % count) for i in range(ends)]),
                cells,
                lax.ppermute(head, axis, [((i + 1) % count, i) for i in range(ends)]),
            ],
            axis=dim,
        )
    return cells


def gll_second():
    gll_nodes = np.array([-1.0, -1.0 / np.sqrt(5.0), 1.0 / np.sqrt(5.0), 1.0])
    npoints = gll_nodes.shape[0]
    bary_weights = np.array(
        [
            1.0
            / np.prod(
                [
                    gll_nodes[col_idx] - gll_nodes[other]
                    for other in range(npoints)
                    if other != col_idx
                ]
            )
            for col_idx in range(npoints)
        ]
    )
    derivative = np.zeros((npoints, npoints))
    for row_idx in range(npoints):
        for col_idx in range(npoints):
            if row_idx != col_idx:
                derivative[row_idx, col_idx] = (
                    bary_weights[col_idx]
                    / bary_weights[row_idx]
                    / (gll_nodes[row_idx] - gll_nodes[col_idx])
                )
        derivative[row_idx, row_idx] = -np.sum(derivative[row_idx])
    return (derivative @ derivative).astype(np.float32)


def pair_average(padded, dim_index):
    length = padded.shape[dim_index] - 2
    middle = lax.slice_in_dim(padded, 1, length + 1, axis=dim_index)
    lower = lax.slice_in_dim(padded, 0, length, axis=dim_index)
    upper = lax.slice_in_dim(padded, 2, length + 2, axis=dim_index)
    bcast_shape = [1] * padded.ndim
    bcast_shape[dim_index] = length
    position = (jnp.arange(length) % NP).reshape(bcast_shape)
    return jnp.where(
        position == 0,
        (middle + lower) * 0.5,
        jnp.where(position == NP - 1, (middle + upper) * 0.5, middle),
    )


def body(
    atm_state,
    ocean_state,
    coupling,
    down_weights,
    down_src,
    down_row,
    down_blk,
    up_weights,
    up_dst,
    up_src,
):
    row_count = lax.axis_size("rows")
    entry_count = up_src.shape[1]
    slot_count = max(2, 2 * entry_count // row_count)
    block_len = down_weights.shape[2]
    field_count = atm_state.shape[0]
    atm_x = atm_state.shape[2]
    atm_y = atm_state.shape[3]
    sea_x = ocean_state.shape[2]
    sea_y = ocean_state.shape[3]
    atm_blocks = atm_x * atm_y // block_len
    sea_blocks = sea_x * sea_y // block_len
    padded_sea = with_halo(ocean_state, ((("comp", "rows"), 2), ("cols", 3)), 1, False)
    surface = ocean_state[:, 0]
    requests = up_src[0]
    whole = lax.all_gather(surface, "rows", axis=1, tiled=True)
    selector = (requests[:, None] == jnp.arange(row_count * sea_blocks)[None, :]).astype(
        jnp.float32
    )
    picked = jnp.einsum("bs,fsk->bfk", selector, whole, precision=EXACT)
    remapped = jnp.einsum(
        "bij,bfj->bfi", up_weights[0].astype(jnp.float32), picked, precision=EXACT
    )
    to_atm = (up_dst[0][:, None] == jnp.arange(atm_blocks)[None, :]).astype(jnp.float32)
    sea_at_atm = jnp.einsum("ba,bfi->fai", to_atm, remapped, precision=EXACT)
    flux_atm = coupling * (sea_at_atm - atm_state[:, -1])
    pick_source = (down_src[0][:, None] == jnp.arange(atm_blocks)[None, :]).astype(jnp.float32)
    chosen = jnp.einsum("ba,fak->bfk", pick_source, flux_atm, precision=EXACT)
    partial_value = jnp.einsum(
        "bij,bfj->bfi", down_weights[0].astype(jnp.float32), chosen, precision=EXACT
    )
    target = down_row[0]
    entry = jnp.arange(target.shape[0])
    earlier = (target[:, None] == target[None, :]) & (entry[None, :] < entry[:, None])
    slot_down = jnp.sum(earlier.astype(jnp.int32), axis=1)
    placing = (
        (target * slot_count + slot_down)[:, None] == jnp.arange(row_count * slot_count)[None, :]
    ).astype(jnp.float32)
    sending = jnp.einsum("bs,bfk->sfk", placing, partial_value, precision=EXACT).reshape(
        row_count, slot_count, field_count, block_len
    )
    labels = jnp.dot(placing.T, (down_blk[0] + 1).astype(jnp.float32), precision=EXACT) - 1.0
    labels = labels.reshape(row_count, slot_count)
    arrived, arrived_labels = (
        lax.all_to_all(sending, "rows", split_axis=0, concat_axis=0, tiled=True),
        lax.all_to_all(labels, "rows", split_axis=0, concat_axis=0, tiled=True),
    )
    taking = (
        arrived_labels.reshape(-1)[None, :] == jnp.arange(sea_blocks).astype(jnp.float32)[:, None]
    ).astype(jnp.float32)
    flux_sea = jnp.einsum(
        "os,sfk->fok",
        taking,
        arrived.reshape(row_count * slot_count, field_count, block_len),
        precision=EXACT,
    )
    second = gll_second()
    kron_x = jnp.asarray(np.kron(np.eye(atm_x // NP, dtype=np.float32), second))
    kron_y = jnp.asarray(np.kron(np.eye(atm_y // NP, dtype=np.float32), second))
    diff_x = jnp.einsum("xz,flzy->flxy", kron_x, atm_state, precision=EXACT)
    diff_y = jnp.einsum("flxz,yz->flxy", atm_state, kron_y, precision=EXACT)
    updated = atm_state + VISCOSITY * (diff_x + diff_y)
    updated = updated.at[:, -1].add(ATM_GAIN * flux_atm)
    across = with_halo(updated, ((("comp", "rows"), 2),), 1, True)
    first_pass = pair_average(across, 2)
    along_cols = with_halo(first_pass, (("cols", 3),), 1, True)
    atm_out = pair_average(along_cols, 3)
    stencil = (
        padded_sea[:, :, 2:, 1:-1]
        + padded_sea[:, :, :-2, 1:-1]
        + padded_sea[:, :, 1:-1, 2:]
        + padded_sea[:, :, 1:-1, :-2]
        - 4.0 * ocean_state
    )
    ocean_out = ocean_state + DIFFUSION * stencil
    ocean_out = ocean_out.at[:, 0].add(SEA_GAIN * flux_sea)
    return (atm_out, ocean_out)


def solution(mesh):
    return jax.shard_map(
        body,
        mesh=mesh,
        in_specs=(
            P(None, None, ("comp", "rows"), "cols"),
            P(None, None, ("comp", "rows"), "cols"),
            P(("comp", "rows"), "cols"),
            P(("comp", "rows"), "cols", None, None),
            P(("comp", "rows"), "cols"),
            P(("comp", "rows"), "cols"),
            P(("comp", "rows"), "cols"),
            P(("comp", "rows"), "cols", None, None),
            P(("comp", "rows"), "cols"),
            P(("comp", "rows"), "cols"),
        ),
        out_specs=(
            P(None, None, ("comp", "rows"), "cols"),
            P(None, None, ("comp", "rows"), "cols"),
        ),
        check_vma=False,
    )
```

profile of v0, /device:TPU:1, one launch (start us, length us, event | category | flops | bytes accessed | tf_op | source)
XLA Modules:
  0.0 62.0 jit_solution(13136688758046114190)
XLA Ops:
  0.6 1.1 %copy.35 = f32[4,8,16,128]{3,2,0,1:T(8,128)S(1)} copy(f32[4,8,16,128]{3,2,1,0:T(8,128)} %param.17) | data formatting | bytes 524288 | tf_op args[1]
  1.7 12.1 %all-gather = f32[4,1,64,128]{3,2,0,1:T(8,128)S(1)} all-gather(f32[4,1,16,128]{3,2,0,1:T(8,128)S(1)} %slice.137), channel_id=2, replica_groups=mesh['comp'=2,'rows'=4,'cols'=4] {'rows'}, dimensions={2}, use_global_device_ids=true | all-gather | bytes 163840 | tf_op jit(solution)/shard_map/all_gather | solution.py:104
  13.8 0.7 %copy-done.7 = s32[1,32]{1,0:T(1,128)S(1)} copy-done((s32[1,32]{1,0:T(1,128)S(1)}, s32[1,32]{1,0:T(1,128)}, u32[]{:S(2)}) %copy-start.7) | copy-done | bytes 152
  14.5 0.2 fusion.31
  14.7 1.7 %fusion.11 = f32[32,4,128]{2,1,0:T(4,128)S(1)} fusion(bf16[1,32,128,128]{3,2,1,0:T(8,128)(2,1)S(1)} %copy-done, f32[32,4,128]{2,0,1:T(8,128)S(1)} %fusion.31), kind=kOutput, calls=%fused_computation.16 | convolution fusion | flops 25165824 | bytes 1179648 | tf_op jit(solution)/shard_map/bij,bfj->bfi/dot_general | solution.py:109
  16.5 0.4 convolution_bitcast_fusion.1
  16.9 0.4 fusion.2
  17.3 0.3 copy-done.6
  17.8 0.7 %collective-permute-start = (f32[4,4,1,128]{3,2,1,0:T(1,128)S(1)}, f32[4,4,1,128]{3,2,1,0:T(1,128)S(1)}, u32[]{:S(2)}, u32[]{:S(2)}) collective-permute-start(f32[4,4,1,128]{3,2,1,0:T(1,128)S(1)} %get-tuple-element.38), channel_id=1, source_target_pairs={{0,4},{4,8},{8,12},{12,16},{16,20},{20,24},{24,28},{28,0},{1,5},{5... | collective-permute-start | bytes 24584 | tf_op jit(solution)/shard_map/ppermute | solution.py:25
  18.5 3.5 %collective-permute-start.1 = (f32[4,4,1,128]{3,2,1,0:T(1,128)S(1)}, f32[4,4,1,128]{3,2,1,0:T(1,128)S(1)}, u32[]{:S(2)}, u32[]{:S(2)}) collective-permute-start(f32[4,4,1,128]{3,2,1,0:T(1,128)S(1)} %get-tuple-element.39), channel_id=1, source_target_pairs={{4,0},{8,4},{12,8},{16,12},{20,16},{24,20},{28,24},{0,28},{5,1},{9... | collective-permute-start | bytes 24584 | tf_op jit(solution)/shard_map/ppermute | solution.py:27
  22.0 1.3 %collective-permute-start.4 = (f32[4,8,1,128]{3,2,0,1:T(1,128)S(1)}, f32[4,8,1,128]{3,2,0,1:T(1,128)S(1)}, u32[]{:S(2)}, u32[]{:S(2)}) collective-permute-start(f32[4,8,1,128]{3,2,0,1:T(1,128)S(1)} %get-tuple-element.35), channel_id=1, source_target_pairs={{4,0},{8,4},{12,8},{16,12},{20,16},{24,20},{28,24},{5,1},{9,5},{13... | collective-permute-start | bytes 49160 | tf_op jit(solution)/shard_map/ppermute | solution.py:27
  23.3 4.0 %collective-permute-start.5 = (f32[4,8,1,128]{3,2,0,1:T(1,128)S(1)}, f32[4,8,1,128]{3,2,0,1:T(1,128)S(1)}, u32[]{:S(2)}, u32[]{:S(2)}) collective-permute-start(f32[4,8,1,128]{3,2,0,1:T(1,128)S(1)} %get-tuple-element.34), channel_id=1, source_target_pairs={{0,4},{4,8},{8,12},{12,16},{16,20},{20,24},{24,28},{1,5},{5,9},{9,... | collective-permute-start | bytes 49160 | tf_op jit(solution)/shard_map/ppermute | solution.py:25
  27.5 0.6 %copy-done.11 = s32[1,32]{1,0:T(1,128)S(1)} copy-done((s32[1,32]{1,0:T(1,128)S(1)}, s32[1,32]{1,0:T(1,128)}, u32[]{:S(2)}) %copy-start.11) | copy-done | bytes 152
  28.3 0.7 %all_to_all.10 = f32[4,1,16]{2,0,1:T(4,128)} reshape(f32[64]{0:T(128)S(1)} %fusion.8) | data formatting | bytes 512 | tf_op jit(solution)/shard_map/all_to_all | solution.py:134
  29.0 4.0 %all-to-all-start.1 = ((f32[4,1,16]{2,1,0:T(1,128)}), f32[4,1,16]{2,1,0:T(1,128)S(1)}, u32[]{:S(2)}, u32[]{:S(2)}) async-start(f32[4,1,16]{2,1,0:T(1,128)} %bitcast.25), calls=%async_computation.1 | async-start | bytes 4096 | tf_op jit(solution)/shard_map/all_to_all | solution.py:134
  33.0 0.6 %copy-done.9 = s32[1,32]{1,0:T(1,128)S(1)} copy-done((s32[1,32]{1,0:T(1,128)S(1)}, s32[1,32]{1,0:T(1,128)}, u32[]{:S(2)}) %copy-start.9) | copy-done | bytes 152
  33.7 0.2 fusion.48
  33.9 1.7 %fusion.9 = f32[32,4,128]{2,1,0:T(4,128)S(1)} fusion(bf16[1,32,128,128]{3,2,1,0:T(8,128)(2,1)S(1)} %copy-done.3, f32[32,4,128]{2,0,1:T(8,128)S(1)} %fusion.48), kind=kOutput, calls=%fused_computation.14 | convolution fusion | flops 25165824 | bytes 1179648 | tf_op jit(solution)/shard_map/bij,bfj->bfi/dot_general | solution.py:117
  35.6 0.3 fusion.34
  36.0 0.7 %copy.48 = f32[4,16,4,128]{3,1,2,0:T(8,128)} copy(f32[4,16,4,128]{3,1,0,2:T(8,128)S(1)} %bitcast.85) | data formatting | bytes 262144 | tf_op jit(solution)/shard_map/reshape | solution.py:127
  36.7 0.7 %all-to-all-done.1 = f32[4,1,16]{2,1,0:T(1,128)S(1)} async-done(((f32[4,1,16]{2,1,0:T(1,128)}), f32[4,1,16]{2,1,0:T(1,128)S(1)}, u32[]{:S(2)}, u32[]{:S(2)}) %all-to-all-start.1) | async-done | bytes 288 | tf_op jit(solution)/shard_map/all_to_all | solution.py:134
  37.4 3.8 %all-to-all-start = ((f32[4,16,4,128]{3,1,2,0:T(8,128)}), f32[4,16,4,128]{3,1,2,0:T(8,128)S(1)}, u32[]{:S(2)}, u32[]{:S(2)}) async-start(f32[4,16,4,128]{3,1,2,0:T(8,128)} %copy.48), calls=%async_computation | async-start | bytes 262144 | tf_op jit(solution)/shard_map/all_to_all | solution.py:133
  41.2 0.5 broadcast.151
  41.7 0.7 %reduce.7 = f32[4,16]{1,0:T(4,128)S(1)} reduce(f32[4,1,16]{2,1,0:T(1,128)S(1)} %all-to-all-done.1, f32[]{:T(128)} %broadcast.151), dimensions={1}, to_apply=%all_to_all.11.reduce_sub_computation.3 | reduce | bytes 516 | tf_op jit(solution)/shard_map/all_to_all | solution.py:134
  42.7 6.9 %collective-permute-start.2 = (f32[4,4,32,1]{3,2,1,0:T(8,128)S(1)}, f32[4,4,32,1]{3,2,1,0:T(8,128)S(1)}, u32[]{:S(2)}, u32[]{:S(2)}) collective-permute-start(f32[4,4,32,1]{3,2,1,0:T(8,128)S(1)} %get-tuple-element.36), channel_id=1, source_target_pairs={{0,1},{1,2},{2,3},{3,0},{4,5},{5,6},{6,7},{7,4},{8,9},{9,10},{10,1... | collective-permute-start | bytes 6152 | tf_op jit(solution)/shard_map/ppermute | solution.py:25
  49.9 2.5 %collective-permute-start.6 = (f32[4,8,18,1]{3,2,0,1:T(8,128)S(1)}, f32[4,8,18,1]{3,2,0,1:T(8,128)S(1)}, u32[]{:S(2)}, u32[]{:S(2)}) collective-permute-start(f32[4,8,18,1]{3,2,0,1:T(8,128)S(1)} %get-tuple-element.32), channel_id=1, source_target_pairs={{1,0},{2,1},{3,2},{5,4},{6,5},{7,6},{9,8},{10,9},{11,10},{13,12},{... | collective-permute-start | bytes 6920 | tf_op jit(solution)/shard_map/ppermute | solution.py:27
  52.5 3.0 %collective-permute-start.7 = (f32[4,8,18,1]{3,2,0,1:T(8,128)S(1)}, f32[4,8,18,1]{3,2,0,1:T(8,128)S(1)}, u32[]{:S(2)}, u32[]{:S(2)}) collective-permute-start(f32[4,8,18,1]{3,2,0,1:T(8,128)S(1)} %get-tuple-element.33), channel_id=1, source_target_pairs={{0,1},{1,2},{2,3},{4,5},{5,6},{6,7},{8,9},{9,10},{10,11},{12,13},{... | collective-permute-start | bytes 6920 | tf_op jit(solution)/shard_map/ppermute | solution.py:25
  55.5 0.9 %collective-permute-done.3 = f32[4,4,32,1]{3,2,1,0:T(8,128)S(1)} collective-permute-done((f32[4,4,32,1]{3,2,1,0:T(8,128)S(1)}, f32[4,4,32,1]{3,2,1,0:T(8,128)S(1)}, u32[]{:S(2)}, u32[]{:S(2)}) %collective-permute-start.3) | collective-permute-done | bytes 2080 | tf_op jit(solution)/shard_map/ppermute | solution.py:27
  56.5 1.0 %fusion.22 = f32[4,4,32,128]{3,2,1,0:T(8,128)} fusion(f32[4,4,32,128]{3,2,1,0:T(8,128)S(1)} %fusion.28, f32[4,4,32,1]{3,2,1,0:T(8,128)S(1)} %collective-permute-done.3, f32[4,4,32,1]{3,2,1,0:T(8,128)S(1)} %collective-permute-done.2, pred[128]{0:T(512)(128)(4,1)S(1)} %get-tuple-element.45, pred[128]{0:T(512)(128)(4,1)S(1)} %get-tuple-element.44), kind=kLoop, calls=%fused_computation.37 | loop fusion | flops 524288 | bytes 528640 | tf_op jit(solution)/shard_map/jit(_where)/select_n | solution.py:71
  57.4 3.2 %collective-permute-done.6 = f32[4,8,18,1]{3,2,0,1:T(8,128)S(1)} collective-permute-done((f32[4,8,18,1]{3,2,0,1:T(8,128)S(1)}, f32[4,8,18,1]{3,2,0,1:T(8,128)S(1)}, u32[]{:S(2)}, u32[]{:S(2)}) %collective-permute-start.6) | collective-permute-done | bytes 2336 | tf_op jit(solution)/shard_map/ppermute | solution.py:27
  60.7 0.3 fusion.16
  61.3 0.7 %copy.51 = f32[4,8,16,128]{3,2,1,0:T(8,128)} copy(f32[4,8,16,128]{3,2,0,1:T(8,128)S(1)} %fusion.7) | data formatting | bytes 524288
  (45 shorter events, 1.4 us)
Async XLA Ops:
  0.6 14.1 %copy-start = (bf16[1,32,128,128]{3,2,1,0:T(8,128)(2,1)S(1)}, bf16[1,32,128,128]{3,2,1,0:T(8,128)(2,1)}, u32[]{:S(2)}) copy-start(bf16[1,32,128,128]{3,2,1,0:T(8,128)(2,1)} %param.23) | copy-start | bytes 3145732
  13.8 0.7 %copy-start.7 = (s32[1,32]{1,0:T(1,128)S(1)}, s32[1,32]{1,0:T(1,128)}, u32[]{:S(2)}) copy-start(s32[1,32]{1,0:T(1,128)} %param.25) | copy-start | bytes 388
  14.7 1.8 %copy-start.1 = (f32[4,4,32,128]{3,2,1,0:T(8,128)S(1)}, f32[4,4,32,128]{3,2,1,0:T(8,128)}, u32[]{:S(2)}) copy-start(f32[4,4,32,128]{3,2,1,0:T(8,128)} %param.16) | copy-start | bytes 786436
  14.7 1.7 %copy-start.5 = (f32[32,32,1,1]{1,0,3,2:T(8,128)S(1)}, f32[32,32,1,1]{1,0,3,2:T(8,128)}, u32[]{:S(2)}) copy-start(f32[32,32,1,1]{1,0,3,2:T(8,128)} %constant.113) | copy-start | bytes 12292
  14.7 2.1 %copy-start.4 = (f32[128,128,1,1]{1,0,3,2:T(8,128)S(1)}, f32[128,128,1,1]{1,0,3,2:T(8,128)}, u32[]{:S(2)}) copy-start(f32[128,128,1,1]{1,0,3,2:T(8,128)} %constant.114) | copy-start | bytes 196612
  16.5 17.4 %copy-start.3 = (bf16[1,32,128,128]{3,2,1,0:T(8,128)(2,1)S(1)}, bf16[1,32,128,128]{3,2,1,0:T(8,128)(2,1)}, u32[]{:S(2)}) copy-start(bf16[1,32,128,128]{3,2,1,0:T(8,128)(2,1)} %param.19) | copy-start | bytes 3145732
  16.9 0.7 %copy-start.6 = (f32[32,128]{1,0:T(8,128)S(1)}, f32[32,128]{1,0:T(8,128)}, u32[]{:S(2)}) copy-start(f32[32,128]{1,0:T(8,128)} %param.18) | copy-start | bytes 49156
  16.9 0.7 %copy-start.8 = (s32[1,32]{1,0:T(1,128)S(1)}, s32[1,32]{1,0:T(1,128)}, u32[]{:S(2)}) copy-start(s32[1,32]{1,0:T(1,128)} %param.24) | copy-start | bytes 388
  17.3 4.7 %copy-start.2 = (f32[4,8,16,128]{3,2,1,0:T(8,128)S(1)}, f32[4,8,16,128]{3,2,1,0:T(8,128)}, u32[]{:S(2)}) copy-start(f32[4,8,16,128]{3,2,1,0:T(8,128)} %param.17) | copy-start | bytes 786436
  17.8 24.7 %collective-permute-start = (f32[4,4,1,128]{3,2,1,0:T(1,128)S(1)}, f32[4,4,1,128]{3,2,1,0:T(1,128)S(1)}, u32[]{:S(2)}, u32[]{:S(2)}) collective-permute-start(f32[4,4,1,128]{3,2,1,0:T(1,128)S(1)} %get-tuple-element.38), channel_id=1, source_target_pairs={{0,4},{4,8},{8,12},{12,16},{16,20},{20,24},{24,28},{28,0},{1,5},{5... | collective-permute-start | bytes 24584 | tf_op jit(solution)/shard_map/ppermute | solution.py:25
  18.5 23.9 %collective-permute-start.1 = (f32[4,4,1,128]{3,2,1,0:T(1,128)S(1)}, f32[4,4,1,128]{3,2,1,0:T(1,128)S(1)}, u32[]{:S(2)}, u32[]{:S(2)}) collective-permute-start(f32[4,4,1,128]{3,2,1,0:T(1,128)S(1)} %get-tuple-element.39), channel_id=1, source_target_pairs={{4,0},{8,4},{12,8},{16,12},{20,16},{24,20},{28,24},{0,28},{5,1},{9... | collective-permute-start | bytes 24584 | tf_op jit(solution)/shard_map/ppermute | solution.py:27
  22.0 27.6 %collective-permute-start.4 = (f32[4,8,1,128]{3,2,0,1:T(1,128)S(1)}, f32[4,8,1,128]{3,2,0,1:T(1,128)S(1)}, u32[]{:S(2)}, u32[]{:S(2)}) collective-permute-start(f32[4,8,1,128]{3,2,0,1:T(1,128)S(1)} %get-tuple-element.35), channel_id=1, source_target_pairs={{4,0},{8,4},{12,8},{16,12},{20,16},{24,20},{28,24},{5,1},{9,5},{13... | collective-permute-start | bytes 49160 | tf_op jit(solution)/shard_map/ppermute | solution.py:27
  23.3 4.0 %copy-start.10 = (s32[1,32]{1,0:T(1,128)S(1)}, s32[1,32]{1,0:T(1,128)}, u32[]{:S(2)}) copy-start(s32[1,32]{1,0:T(1,128)} %param.21) | copy-start | bytes 388
  23.3 26.3 %collective-permute-start.5 = (f32[4,8,1,128]{3,2,0,1:T(1,128)S(1)}, f32[4,8,1,128]{3,2,0,1:T(1,128)S(1)}, u32[]{:S(2)}, u32[]{:S(2)}) collective-permute-start(f32[4,8,1,128]{3,2,0,1:T(1,128)S(1)} %get-tuple-element.34), channel_id=1, source_target_pairs={{0,4},{4,8},{8,12},{12,16},{16,20},{20,24},{24,28},{1,5},{5,9},{9,... | collective-permute-start | bytes 49160 | tf_op jit(solution)/shard_map/ppermute | solution.py:25
  27.5 0.7 %copy-start.11 = (s32[1,32]{1,0:T(1,128)S(1)}, s32[1,32]{1,0:T(1,128)}, u32[]{:S(2)}) copy-start(s32[1,32]{1,0:T(1,128)} %param.22) | copy-start | bytes 388
  29.0 8.4 %all-to-all-start.1 = ((f32[4,1,16]{2,1,0:T(1,128)}), f32[4,1,16]{2,1,0:T(1,128)S(1)}, u32[]{:S(2)}, u32[]{:S(2)}) async-start(f32[4,1,16]{2,1,0:T(1,128)} %bitcast.25), calls=%async_computation.1 | async-start | bytes 4096 | tf_op jit(solution)/shard_map/all_to_all | solution.py:134
  33.0 0.7 %copy-start.9 = (s32[1,32]{1,0:T(1,128)S(1)}, s32[1,32]{1,0:T(1,128)}, u32[]{:S(2)}) copy-start(s32[1,32]{1,0:T(1,128)} %param.20) | copy-start | bytes 388
  37.4 23.7 %all-to-all-start = ((f32[4,16,4,128]{3,1,2,0:T(8,128)}), f32[4,16,4,128]{3,1,2,0:T(8,128)S(1)}, u32[]{:S(2)}, u32[]{:S(2)}) async-start(f32[4,16,4,128]{3,1,2,0:T(8,128)} %copy.48), calls=%async_computation | async-start | bytes 262144 | tf_op jit(solution)/shard_map/all_to_all | solution.py:133
  42.7 12.8 %collective-permute-start.2 = (f32[4,4,32,1]{3,2,1,0:T(8,128)S(1)}, f32[4,4,32,1]{3,2,1,0:T(8,128)S(1)}, u32[]{:S(2)}, u32[]{:S(2)}) collective-permute-start(f32[4,4,32,1]{3,2,1,0:T(8,128)S(1)} %get-tuple-element.36), channel_id=1, source_target_pairs={{0,1},{1,2},{2,3},{3,0},{4,5},{5,6},{6,7},{7,4},{8,9},{9,10},{10,1... | collective-permute-start | bytes 6152 | tf_op jit(solution)/shard_map/ppermute | solution.py:25
  49.7 6.8 %collective-permute-start.3 = (f32[4,4,32,1]{3,2,1,0:T(8,128)S(1)}, f32[4,4,32,1]{3,2,1,0:T(8,128)S(1)}, u32[]{:S(2)}, u32[]{:S(2)}) collective-permute-start(f32[4,4,32,1]{3,2,1,0:T(8,128)S(1)} %get-tuple-element.37), channel_id=1, source_target_pairs={{1,0},{2,1},{3,2},{0,3},{5,4},{6,5},{7,6},{4,7},{9,8},{10,9},{11,1... | collective-permute-start | bytes 6152 | tf_op jit(solution)/shard_map/ppermute | solution.py:27
  49.9 10.7 %collective-permute-start.6 = (f32[4,8,18,1]{3,2,0,1:T(8,128)S(1)}, f32[4,8,18,1]{3,2,0,1:T(8,128)S(1)}, u32[]{:S(2)}, u32[]{:S(2)}) collective-permute-start(f32[4,8,18,1]{3,2,0,1:T(8,128)S(1)} %get-tuple-element.32), channel_id=1, source_target_pairs={{1,0},{2,1},{3,2},{5,4},{6,5},{7,6},{9,8},{10,9},{11,10},{13,12},{... | collective-permute-start | bytes 6920 | tf_op jit(solution)/shard_map/ppermute | solution.py:27
  52.5 8.2 %collective-permute-start.7 = (f32[4,8,18,1]{3,2,0,1:T(8,128)S(1)}, f32[4,8,18,1]{3,2,0,1:T(8,128)S(1)}, u32[]{:S(2)}, u32[]{:S(2)}) collective-permute-start(f32[4,8,18,1]{3,2,0,1:T(8,128)S(1)} %get-tuple-element.33), channel_id=1, source_target_pairs={{0,1},{1,2},{2,3},{4,5},{5,6},{6,7},{8,9},{9,10},{10,11},{12,13},{... | collective-permute-start | bytes 6920 | tf_op jit(solution)/shard_map/ppermute | solution.py:25
where the time goes:
time: 62.4 us; the launch traced here: 62 us
  starting transfers between devices  29.8 us (48%)
  blocking collectives  12.1 us (19%)
  local copies, waits for them, and re-layouts  6.43 us (10%)
  matrix products  5.43 us (9%)
  waiting for transfers between devices  4.9 us (8%)
  other arithmetic  2.38 us (4%)
  between operations  0.94 us (2%)
    ppermute x4, starting transfers between devices, with_halo(): lax.ppermute(tail, axis, [(i, (i + 1) % count) for i in range(ends)])  14.7 us
    all_gather x1, blocking collectives, body(): whole = lax.all_gather(surface, 'rows', axis=1, tiled=True)  12.1 us
    ppermute x4, starting transfers between devices, with_halo(): lax.ppermute(head, axis, [((i + 1) % count, i) for i in range(ends)])  7.29 us
    ppermute x4, waiting for transfers between devices, with_halo(): lax.ppermute(head, axis, [((i + 1) % count, i) for i in range(ends)])  4.18 us
    unnamed x26, local copies, waits for them, and re-layouts  4.1 us
    all_to_all x1, starting transfers between devices, body(): lax.all_to_all(labels, 'rows', split_axis=0, concat_axis=0, tiled=True)  4.01 us
    all_to_all x1, starting transfers between devices, body(): lax.all_to_all(sending, 'rows', split_axis=0, concat_axis=0, tiled=True)  3.82 us
    dot_general x1, matrix products, body(): jnp.einsum('bij,bfj->bfi', up_weights[0].astype(jnp.float32), picked, pre...  1.72 us
  transfers between devices with their start and end apart: 10, of which 3 were waited for; matrix products, arithmetic and copies ran while one was open for 10% of the time, Pallas kernels for 0%

commit v1 on v0

v1 whole, which is shorter than its diff:
```python
import functools

import jax
import jax.numpy as jnp
import numpy as np
from jax import lax
from jax.experimental import pallas as pl
from jax.experimental.pallas import tpu as pltpu
from jax.sharding import PartitionSpec as P

NP = 4
VISCOSITY = 0.01
ATM_GAIN = 0.5
DIFFUSION = 0.1
SEA_GAIN = 0.5
MESH = pl.DeviceIdType.MESH
F32 = jnp.float32
BF16 = jnp.bfloat16


def gll_second():
    gll_nodes = np.array([-1.0, -1.0 / np.sqrt(5.0), 1.0 / np.sqrt(5.0), 1.0])
    n = gll_nodes.shape[0]
    bary = np.array(
        [1.0 / np.prod([gll_nodes[c] - gll_nodes[o] for o in range(n) if o != c]) for c in range(n)]
    )
    derivative = np.zeros((n, n))
    for r in range(n):
        for c in range(n):
            if r != c:
                derivative[r, c] = bary[c] / bary[r] / (gll_nodes[r] - gll_nodes[c])
        derivative[r, r] = -np.sum(derivative[r])
    return derivative @ derivative


def iota(shape, dim):
    return lax.broadcasted_iota(jnp.int32, shape, dim)


def bits(n):
    assert n & (n - 1) == 0
    return n.bit_length() - 1


def split(x):
    hi = x.astype(BF16)
    return hi, (x - hi.astype(F32)).astype(BF16)


def dot(a, b):
    return jnp.dot(a, b, preferred_element_type=F32)


def dot_t(a, b):
    return lax.dot_general(a, b, (((1,), (1,)), ((), ())), preferred_element_type=F32)


def kernel(
    sizes,
    atm, oce, coup, dw, dsrc, drow, dblk, uw, udst, usrc,
    aout, oout,
    av, ov, cv, dwv, uwv, in_sem,
    land, land_s, land_r,
    oxs, oxr, oys, oyr, axs, axr, ays, ayr, fxs, fxr, fys, fyr, halo_s, halo_r,
    dns, dnr, dn_s, dn_r,
    ub, aov, oov, flb, sel_u, t_u, sel_d, t_d, picked, rem, out_sem,
):
    comps, rows, cols = sizes
    c = lax.axis_index("comp")
    r = lax.axis_index("rows")
    k = lax.axis_index("cols")
    nf, al, ax, ln = av.shape
    ol, ox = ov.shape[1], ov.shape[2]
    nb = dsrc.shape[1]
    group = 2 * nf
    ent = nb * group
    total = comps * rows
    g = c * rows + r

    ins = [
        pltpu.make_async_copy(oce, ov, in_sem.at[0]),
        pltpu.make_async_copy(atm, av, in_sem.at[1]),
        pltpu.make_async_copy(coup, cv, in_sem.at[2]),
        pltpu.make_async_copy(uw.at[0], uwv, in_sem.at[3]),
        pltpu.make_async_copy(dw.at[0], dwv, in_sem.at[4]),
    ]
    for copy in ins:
        copy.start()

    def x_neighbour(step):
        other = lax.rem(g + step + total, total)
        return {"comp": other // rows, "rows": lax.rem(other, rows)}

    def y_neighbour(step):
        return {"cols": lax.rem(k + step + cols, cols)}

    def row_peer(step):
        return {"rows": lax.rem(r + step, rows)}

    partners = [x_neighbour(-1), x_neighbour(1), y_neighbour(-1), y_neighbour(1)]
    partners += [row_peer(d) for d in range(1, rows)]
    barrier = pltpu.get_barrier_semaphore()
    for who in partners:
        pl.semaphore_signal(barrier, inc=1, device_id=who, device_id_type=MESH)

    lane = iota((1, ln), 1)

    ins[0].wait()
    west = jnp.zeros((ox, ln), F32)
    east = jnp.zeros((ox, ln), F32)
    for f in range(nf):
        for l in range(ol):
            q = f * ol + l
            tile = ov[f, l]
            oxs[0, q : q + 1, :] = tile[0:1, :]
            oxs[1, q : q + 1, :] = tile[ox - 1 : ox, :]
            west = jnp.where(lane == q, tile[:, 0:1], west)
            east = jnp.where(lane == q, tile[:, ln - 1 : ln], east)
    oys[0] = west
    oys[1] = east

    pl.semaphore_wait(barrier, len(partners))

    def send(src, dst, s_sem, r_sem, who):
        copy = pltpu.make_async_remote_copy(
            src_ref=src, dst_ref=dst, send_sem=s_sem, recv_sem=r_sem,
            device_id=who, device_id_type=MESH,
        )
        copy.start()
        return copy

    def exchange(which, src, dst, neighbour):
        return [
            send(src.at[i], dst.at[i], halo_s.at[which, i], halo_r.at[which, i], neighbour(step))
            for i, step in enumerate((-1, 1))
        ]

    order = sorted(range(1, rows), key=lambda d: -min(d, rows - d))
    surface = [
        send(ov.at[:, 0], land.at[d], land_s.at[d], land_r.at[d], row_peer(d)) for d in order
    ]
    sea_x = exchange(0, oxs, oxr, x_neighbour)
    sea_y = exchange(1, oys, oyr, y_neighbour)
    land[0] = ov[:, 0]

    second = gll_second() * VISCOSITY

    def coefficient(position, d):
        out = jnp.zeros(position.shape, F32)
        for i in range(NP):
            if 0 <= i + d < NP:
                out = jnp.where(position == i, float(second[i, i + d]), out)
        return out

    px = iota((8, ln), 0) & (NP - 1)
    py = iota((8, ln), 1) & (NP - 1)
    here = 1.0 + coefficient(px, 0) + coefficient(py, 0)
    steps = [d for d in range(1 - NP, NP) if d]
    cx = {d: coefficient(px, d) for d in steps}
    cy = {d: coefficient(py, d) for d in steps}
    ins[1].wait()
    for f in range(nf):
        for l in range(al):
            q = f * al + l
            for t in range(ax // 8):
                a = av[f, l, 8 * t : 8 * t + 8, :]
                u = here * a
                for d in steps:
                    u += cx[d] * pltpu.roll(a, (-d) % 8, 0)
                    u += cy[d] * pltpu.roll(a, (-d) % ln, 1)
                ub[q, 8 * t : 8 * t + 8, :] = u
                if t == 0:
                    axs[0, q : q + 1, :] = u[0:1, :]
                if t == ax // 8 - 1:
                    axs[1, q : q + 1, :] = u[7:8, :]
    atm_x = exchange(2, axs, axr, x_neighbour)

    def column(ref):
        row = ref[...].astype(F32)
        pick = (iota((ent, nb), 0) >> bits(group)) == iota((ent, nb), 1)
        return jnp.sum(jnp.where(pick, row, 0.0), axis=1, keepdims=True)

    def spread(ref):
        row = ref[...].astype(F32)
        pick = iota((nb, nb), 0) == iota((nb, nb), 1)
        col = jnp.sum(jnp.where(pick, row, 0.0), axis=1, keepdims=True)
        pick = (iota((nb, ent), 1) >> bits(group)) == iota((nb, ent), 0)
        return jnp.sum(jnp.where(pick, col, 0.0), axis=0, keepdims=True)

    def hot(a, b):
        return jnp.where(a == b, 1.0, 0.0).astype(BF16)

    me = r.astype(F32)
    part = iota((ent, 1), 0) & (group - 1)
    part_field = (part & (nf - 1)).astype(F32)
    part_low = (part >> bits(nf)).astype(F32)
    lane_field = (iota((1, ent), 1) & (nf - 1)).astype(F32)

    s = column(usrc)
    owner = jnp.floor(s * (1.0 / ox))
    slot = me - owner
    slot = jnp.where(slot < 0.0, slot + rows, slot)
    key = ((part_low * rows + slot) * nf + part_field) * ox + (s - owner * ox)
    sel_u[...] = hot(key, iota(sel_u.shape, 1).astype(F32))
    t_u[...] = hot(iota(t_u.shape, 0).astype(F32), lane_field * ax + spread(udst))
    key = (part_low * nf + part_field) * ax + column(dsrc)
    sel_d[...] = hot(key, iota(sel_d.shape, 1).astype(F32))
    slot = spread(drow) - me
    slot = jnp.where(slot < 0.0, slot + rows, slot)
    key = (slot * nf + lane_field) * ox + spread(dblk)
    t_d[...] = hot(iota(t_d.shape, 0).astype(F32), key)

    def remap(sel, source, weights, place):
        hi, lo = split(source)
        picked[...] = dot(sel[...], jnp.concatenate([hi, lo], axis=0))
        for b in range(nb):
            rows_b = slice(b * group, (b + 1) * group)
            rem[rows_b, :] = dot_t(picked[rows_b, :].astype(BF16), weights[b])
        hi, lo = split(rem[...])
        both = dot(place[...], jnp.concatenate([hi, lo], axis=1))
        return both[:, :ln] + both[:, ln:]

    ins[2].wait()
    ins[3].wait()
    for copy in surface:
        copy.wait_recv()
    sea = remap(sel_u, land[...].reshape(rows * nf * ox, ln), uwv, t_u)
    flux = cv[...] * (sea.reshape(nf, ax, ln) - av[:, al - 1])
    flb[...] = flux
    for f in range(nf):
        fxs[0, f : f + 1, :] = flb[f, 0:1, :]
        fxs[1, f : f + 1, :] = flb[f, ax - 1 : ax, :]
    flux_x = exchange(4, fxs, fxr, x_neighbour)

    ins[4].wait()
    down = remap(sel_d, flb[...].reshape(nf * ax, ln), dwv, t_d)
    dns[...] = down.reshape(rows, nf, ox, ln)
    going = [send(dns.at[d], dnr.at[d], dn_s.at[d], dn_r.at[d], row_peer(d)) for d in order]

    row_id = iota((ax, ln), 0)
    lane_id = iota((ax, ln), 1)
    first_row, last_row = row_id == 0, row_id == ax - 1
    first_lane, last_lane = lane_id == 0, lane_id == ln - 1
    x_pos, y_pos = row_id & (NP - 1), lane_id & (NP - 1)

    def average(u, axis, before, after):
        first, last, pos = (
            (first_row, last_row, x_pos) if axis == 0 else (first_lane, last_lane, y_pos)
        )
        low = jnp.where(first, before, pltpu.roll(u, 1, axis))
        high = jnp.where(last, after, pltpu.roll(u, u.shape[axis] - 1, axis))
        return jnp.where(
            pos == 0, (u + low) * 0.5, jnp.where(pos == NP - 1, (u + high) * 0.5, u)
        )

    def x_pass(copies, recv, store, packed, count):
        for copy in copies:
            copy.wait_recv()
        west = jnp.zeros((ax, ln), F32)
        east = jnp.zeros((ax, ln), F32)
        for q in range(count):
            e = average(store[q], 0, recv[1, q : q + 1, :], recv[0, q : q + 1, :])
            store[q] = e
            west = jnp.where(lane == q, e[:, 0:1], west)
            east = jnp.where(lane == q, e[:, ln - 1 : ln], east)
        packed[0] = west
        packed[1] = east

    x_pass(atm_x, axr, ub, ays, nf * al)
    atm_y = exchange(3, ays, ayr, y_neighbour)

    for copy in sea_x + sea_y:
        copy.wait_recv()
    o_row = iota((ox, ln), 0)
    o_lane = iota((ox, ln), 1)
    west = jnp.where(k == 0, 0.0, oyr[1])
    east = jnp.where(k == cols - 1, 0.0, oyr[0])

    def stencil(f, l):
        q = f * ol + l
        x = ov[f, l]
        before = jnp.where(g == 0, 0.0, oxr[1, q : q + 1, :])
        after = jnp.where(g == total - 1, 0.0, oxr[0, q : q + 1, :])
        ring = jnp.where(o_row == 0, before, pltpu.roll(x, 1, 0))
        ring += jnp.where(o_row == ox - 1, after, pltpu.roll(x, ox - 1, 0))
        ring += jnp.where(o_lane == 0, west[:, q : q + 1], pltpu.roll(x, 1, 1))
        ring += jnp.where(o_lane == ln - 1, east[:, q : q + 1], pltpu.roll(x, ln - 1, 1))
        oov[f, l] = x + DIFFUSION * (ring - 4.0 * x)

    for f in range(nf):
        for l in range(ol):
            stencil(f, l)
    outs = [pltpu.make_async_copy(oov.at[:, 1:], oout.at[:, 1:], out_sem.at[0])]
    outs[0].start()

    x_pass(flux_x, fxr, flb, fys, nf)
    flux_y = exchange(5, fys, fyr, y_neighbour)

    for copy in atm_y:
        copy.wait_recv()
    before, after = ayr[1], ayr[0]
    for f in range(nf):
        for l in range(al):
            q = f * al + l
            aov[f, l] = average(ub[q], 1, before[:, q : q + 1], after[:, q : q + 1])
    outs.append(pltpu.make_async_copy(aov.at[:, : al - 1], aout.at[:, : al - 1], out_sem.at[1]))
    outs[1].start()

    for copy in flux_y:
        copy.wait_recv()
    before, after = fyr[1], fyr[0]
    for f in range(nf):
        e = average(flb[f], 1, before[:, f : f + 1], after[:, f : f + 1])
        aov[f, al - 1] = aov[f, al - 1] + ATM_GAIN * e
    outs.append(pltpu.make_async_copy(aov.at[:, al - 1], aout.at[:, al - 1], out_sem.at[2]))
    outs[2].start()

    for copy in going:
        copy.wait_recv()
    arrived = dns[0]
    for d in range(1, rows):
        arrived += dnr[d]
    oov[:, 0] = oov[:, 0] + SEA_GAIN * arrived
    outs.append(pltpu.make_async_copy(oov.at[:, 0], oout.at[:, 0], out_sem.at[3]))
    outs[3].start()

    for copy in surface + sea_x + sea_y + atm_x + atm_y + flux_x + flux_y + going:
        copy.wait_send()
    for copy in outs:
        copy.wait()


def body(sizes, atm, oce, coup, dw, dsrc, drow, dblk, uw, udst, usrc):
    rows = sizes[1]
    nf, al, ax, ln = atm.shape
    ol, ox = oce.shape[1], oce.shape[2]
    nb, blk = dw.shape[1], dw.shape[2]
    assert ln == blk and oce.shape[3] == blk
    fa, fo, ent = nf * al, nf * ol, nb * 2 * nf
    assert fa <= ln and fo <= ln
    vm = pltpu.VMEM
    dma = pltpu.SemaphoreType.DMA
    pair = lambda n: [vm((2, n, ln), F32)] * 2
    scratch = [
        vm(atm.shape, F32), vm(oce.shape, F32), vm(coup.shape, F32),
        vm((nb, blk, blk), BF16), vm((nb, blk, blk), BF16), dma((5,)),
        vm((rows, nf, ox, ln), F32), dma((rows,)), dma((rows,)),
        *pair(fo), *pair(ox), *pair(fa), *pair(ax), *pair(nf), *pair(ax),
        dma((6, 2)), dma((6, 2)),
        vm((rows, nf, ox, ln), F32), vm((rows, nf, ox, ln), F32), dma((rows,)), dma((rows,)),
        vm((fa, ax, ln), F32), vm(atm.shape, F32), vm(oce.shape, F32), vm((nf, ax, ln), F32),
        vm((ent, 2 * rows * nf * ox), BF16), vm((nf * ax, ent), BF16),
        vm((ent, 2 * nf * ax), BF16), vm((rows * nf * ox, ent), BF16),
        vm((ent, ln), F32), vm((ent, ln), F32), dma((4,)),
    ]
    hbm = pl.BlockSpec(memory_space=pl.ANY)
    small = pl.BlockSpec(memory_space=pltpu.VMEM)
    return pl.pallas_call(
        functools.partial(kernel, sizes),
        out_shape=(
            jax.ShapeDtypeStruct(atm.shape, F32),
            jax.ShapeDtypeStruct(oce.shape, F32),
        ),
        in_specs=[hbm, hbm, hbm, hbm, small, small, small, hbm, small, small],
        out_specs=(hbm, hbm),
        scratch_shapes=scratch,
        compiler_params=pltpu.CompilerParams(collective_id=0, has_side_effects=True),
        name="coupled_step",
    )(atm, oce, coup, dw, dsrc, drow, dblk, uw, udst, usrc)


def solution(mesh):
    sizes = tuple(mesh.shape[a] for a in ("comp", "rows", "cols"))
    tiles = P(None, None, ("comp", "rows"), "cols")
    flat = P(("comp", "rows"), "cols")
    blocks = P(("comp", "rows"), "cols", None, None)
    return jax.shard_map(
        functools.partial(body, sizes),
        mesh=mesh,
        in_specs=(tiles, tiles, flat, blocks, flat, flat, flat, blocks, flat, flat),
        out_specs=(tiles, tiles),
        check_vma=False,
    )
```

time: 62.4 us -> 23.4 us (0.38)
  starting transfers between devices: 29.8 us -> 0 us
  Pallas kernels: 0 us -> 20.2 us
  blocking collectives: 12.1 us -> 0 us
  matrix products: 5.43 us -> 0 us
  waiting for transfers between devices: 4.9 us -> 0 us
  local copies, waits for them, and re-layouts: 6.43 us -> 2.42 us
  other arithmetic: 2.38 us -> 0 us
    ppermute x8 -> x0, starting transfers between devices: 22 us -> none  [the longest x4 14.7 us: with_halo(): lax.ppermute(tail, axis, [(i, (i + 1) % count) for i in range(ends)])]
    pallas_call x0 -> x1, Pallas kernels: none -> 20.2 us  [body(): pl.pallas_call(functools.partial(kernel, sizes), out_shape=(jax.ShapeDtyp...]
    all_gather x1 -> x0, blocking collectives: 12.1 us -> none  [body(): whole = lax.all_gather(surface, 'rows', axis=1, tiled=True)]
    all_to_all x2 -> x0, starting transfers between devices: 7.83 us -> none  [the longest x1 4.01 us: body(): lax.all_to_all(labels, 'rows', split_axis=0, concat_axis=0, tiled=True)]
    dot_general x10 -> x0, matrix products: 5.43 us -> none  [the longest x1 1.72 us: body(): jnp.einsum('bij,bfj->bfi', up_weights[0].astype(jnp.float32), picked, pre...]
    ppermute x8 -> x0, waiting for transfers between devices: 4.19 us -> none  [the longest x4 4.18 us: with_halo(): lax.ppermute(head, axis, [((i + 1) % count, i) for i in range(ends)])]
    unnamed x26 -> x4, local copies, waits for them, and re-layouts: 4.1 us -> 2.42 us
    all_to_all x3 -> x0, local copies, waits for them, and re-layouts: 1.22 us -> none  [the longest x2 1.21 us: body(): lax.all_to_all(labels, 'rows', split_axis=0, concat_axis=0, tiled=True)]
  transfers between devices with their start and end apart: 10 -> 0, of which waited for: 3 -> 0; matrix products, arithmetic and copies ran while one was open for 10% -> 0% of each run, Pallas kernels for 0% -> 0%
where the time goes in v1:
time: 23.4 us; the launch traced here: 23.2 us
  Pallas kernels  20.2 us (86%)
  local copies, waits for them, and re-layouts  2.42 us (10%)
  between operations  0.65 us (3%)
    pallas_call x1, Pallas kernels, body(): pl.pallas_call(functools.partial(kernel, sizes), out_shape=(jax.ShapeDtyp...  20.2 us
    unnamed x4, local copies, waits for them, and re-layouts  2.42 us

profile of v1, /device:TPU:1, one launch (start us, length us, event | category | flops | bytes accessed | tf_op | source)
XLA Modules:
  0.0 23.2 jit_solution(8819014355037809775)
XLA Ops:
  0.6 20.2 %coupled_step.1 = (f32[4,4,32,128]{3,2,1,0:T(8,128)}, f32[4,8,16,128]{3,2,1,0:T(8,128)}) custom-call(f32[4,4,32,128]{3,2,1,0:T(8,128)} %atm.1, f32[4,8,16,128]{3,2,1,0:T(8,128)} %oce.1, f32[32,128]{1,0:T(8,128)} %coup.1, bf16[1,32,128,128]{3,2,1,0:T(8,128)(2,1)} %dw.1, s32[1,32]{1,0:T(1,128)} %dsrc.1, s32[1,32]{1,0:T(1,128)} %drow.1, s32[1,32]{1,0:T(1,128)} %dblk.1, ...), custom_call_target="tpu_custom_call" | custom-call | tf_op jit(solution)/shard_map/coupled_step/pallas_call | solution.py:358
  20.8 0.0 copy-start
  20.8 1.7 %copy.14 = f32[4,4,32,128]{3,2,1,0:T(8,128)} copy(f32[4,4,32,128]{3,2,1,0:T(8,128)} %get-tuple-element.4) | data formatting | bytes 524288
  22.5 0.0 copy-done
  22.5 0.7 %copy.15 = f32[4,8,16,128]{3,2,1,0:T(8,128)} copy(f32[4,8,16,128]{3,2,1,0:T(8,128)S(1)} %copy-done) | data formatting | bytes 524288
Async XLA Ops:
  20.8 1.7 %copy-start = (f32[4,8,16,128]{3,2,1,0:T(8,128)S(1)}, f32[4,8,16,128]{3,2,1,0:T(8,128)}, u32[]{:S(2)}) copy-start(f32[4,8,16,128]{3,2,1,0:T(8,128)} %get-tuple-element.5) | copy-start | bytes 786436

commit v2 on v1

--- a/solution.py
+++ b/solution.py
@@ -57,13 +57,13 @@
 
 def kernel(
     sizes,
-    atm, oce, coup, dw, dsrc, drow, dblk, uw, udst, usrc,
-    aout, oout,
-    av, ov, cv, dwv, uwv, in_sem,
+    atm, oce, coup, dw, dsrc_h, drow_h, dblk_h, uw, udst_h, usrc_h,
+    aov, oov,
+    av, ov, cv, dwv, uwv, in_sem, usrc, udst, dsrc, drow, dblk,
     land, land_s, land_r,
     oxs, oxr, oys, oyr, axs, axr, ays, ayr, fxs, fxr, fys, fyr, halo_s, halo_r,
     dns, dnr, dn_s, dn_r,
-    ub, aov, oov, flb, sel_u, t_u, sel_d, t_d, picked, rem, out_sem,
+    ub, flb, sel_u, t_u, sel_d, t_d, picked, rem,
 ):
     comps, rows, cols = sizes
     c = lax.axis_index("comp")
@@ -77,6 +77,10 @@
     total = comps * rows
     g = c * rows + r
 
+    pairs = ((usrc_h, usrc), (udst_h, udst), (dsrc_h, dsrc), (drow_h, drow), (dblk_h, dblk))
+    tables = [
+        pltpu.make_async_copy(a, b, in_sem.at[5 + i]) for i, (a, b) in enumerate(pairs)
+    ]
     ins = [
         pltpu.make_async_copy(oce, ov, in_sem.at[0]),
         pltpu.make_async_copy(atm, av, in_sem.at[1]),
@@ -84,7 +88,7 @@
         pltpu.make_async_copy(uw.at[0], uwv, in_sem.at[3]),
         pltpu.make_async_copy(dw.at[0], dwv, in_sem.at[4]),
     ]
-    for copy in ins:
+    for copy in ins[:2] + tables + ins[2:]:
         copy.start()
 
     def x_neighbour(step):
@@ -95,7 +99,7 @@
         return {"cols": lax.rem(k + step + cols, cols)}
 
     def row_peer(step):
-        return {"rows": lax.rem(r + step, rows)}
+        return {"rows": r ^ step}
 
     partners = [x_neighbour(-1), x_neighbour(1), y_neighbour(-1), y_neighbour(1)]
     partners += [row_peer(d) for d in range(1, rows)]
@@ -135,11 +139,10 @@
             for i, step in enumerate((-1, 1))
         ]
 
-    order = sorted(range(1, rows), key=lambda d: -min(d, rows - d))
+    order = range(rows - 1, 0, -1)
     surface = [
         send(ov.at[:, 0], land.at[d], land_s.at[d], land_r.at[d], row_peer(d)) for d in order
     ]
-    sea_x = exchange(0, oxs, oxr, x_neighbour)
     sea_y = exchange(1, oys, oyr, y_neighbour)
     land[0] = ov[:, 0]
 
@@ -173,8 +176,9 @@
                     axs[0, q : q + 1, :] = u[0:1, :]
                 if t == ax // 8 - 1:
                     axs[1, q : q + 1, :] = u[7:8, :]
-    atm_x = exchange(2, axs, axr, x_neighbour)
-
+
+    for copy in tables:
+        copy.wait()
     def column(ref):
         row = ref[...].astype(F32)
         pick = (iota((ent, nb), 0) >> bits(group)) == iota((ent, nb), 1)
@@ -190,7 +194,6 @@
     def hot(a, b):
         return jnp.where(a == b, 1.0, 0.0).astype(BF16)
 
-    me = r.astype(F32)
     part = iota((ent, 1), 0) & (group - 1)
     part_field = (part & (nf - 1)).astype(F32)
     part_low = (part >> bits(nf)).astype(F32)
@@ -198,15 +201,13 @@
 
     s = column(usrc)
     owner = jnp.floor(s * (1.0 / ox))
-    slot = me - owner
-    slot = jnp.where(slot < 0.0, slot + rows, slot)
+    slot = (owner.astype(jnp.int32) ^ r).astype(F32)
     key = ((part_low * rows + slot) * nf + part_field) * ox + (s - owner * ox)
     sel_u[...] = hot(key, iota(sel_u.shape, 1).astype(F32))
     t_u[...] = hot(iota(t_u.shape, 0).astype(F32), lane_field * ax + spread(udst))
     key = (part_low * nf + part_field) * ax + column(dsrc)
     sel_d[...] = hot(key, iota(sel_d.shape, 1).astype(F32))
-    slot = spread(drow) - me
-    slot = jnp.where(slot < 0.0, slot + rows, slot)
+    slot = (spread(drow).astype(jnp.int32) ^ r).astype(F32)
     key = (slot * nf + lane_field) * ox + spread(dblk)
     t_d[...] = hot(iota(t_d.shape, 0).astype(F32), key)
 
@@ -224,6 +225,8 @@
     ins[3].wait()
     for copy in surface:
         copy.wait_recv()
+    atm_x = exchange(2, axs, axr, x_neighbour)
+    sea_x = exchange(0, oxs, oxr, x_neighbour)
     sea = remap(sel_u, land[...].reshape(rows * nf * ox, ln), uwv, t_u)
     flux = cv[...] * (sea.reshape(nf, ax, ln) - av[:, al - 1])
     flb[...] = flux
@@ -290,8 +293,6 @@
     for f in range(nf):
         for l in range(ol):
             stencil(f, l)
-    outs = [pltpu.make_async_copy(oov.at[:, 1:], oout.at[:, 1:], out_sem.at[0])]
-    outs[0].start()
 
     x_pass(flux_x, fxr, flb, fys, nf)
     flux_y = exchange(5, fys, fyr, y_neighbour)
@@ -303,8 +304,6 @@
         for l in range(al):
             q = f * al + l
             aov[f, l] = average(ub[q], 1, before[:, q : q + 1], after[:, q : q + 1])
-    outs.append(pltpu.make_async_copy(aov.at[:, : al - 1], aout.at[:, : al - 1], out_sem.at[1]))
-    outs[1].start()
 
     for copy in flux_y:
         copy.wait_recv()
@@ -312,8 +311,6 @@
     for f in range(nf):
         e = average(flb[f], 1, before[:, f : f + 1], after[:, f : f + 1])
         aov[f, al - 1] = aov[f, al - 1] + ATM_GAIN * e
-    outs.append(pltpu.make_async_copy(aov.at[:, al - 1], aout.at[:, al - 1], out_sem.at[2]))
-    outs[2].start()
 
     for copy in going:
         copy.wait_recv()
@@ -321,12 +318,19 @@
     for d in range(1, rows):
         arrived += dnr[d]
     oov[:, 0] = oov[:, 0] + SEA_GAIN * arrived
-    outs.append(pltpu.make_async_copy(oov.at[:, 0], oout.at[:, 0], out_sem.at[3]))
-    outs[3].start()
 
     for copy in surface + sea_x + sea_y + atm_x + atm_y + flux_x + flux_y + going:
         copy.wait_send()
-    for copy in outs:
+
+
+def write_out(a, o, a_out, o_out, sem):
+    copies = [
+        pltpu.make_async_copy(a, a_out, sem.at[0]),
+        pltpu.make_async_copy(o, o_out, sem.at[1]),
+    ]
+    for copy in copies:
+        copy.start()
+    for copy in copies:
         copy.wait()
 
 
@@ -343,30 +347,43 @@
     pair = lambda n: [vm((2, n, ln), F32)] * 2
     scratch = [
         vm(atm.shape, F32), vm(oce.shape, F32), vm(coup.shape, F32),
-        vm((nb, blk, blk), BF16), vm((nb, blk, blk), BF16), dma((5,)),
+        vm((nb, blk, blk), BF16), vm((nb, blk, blk), BF16), dma((10,)),
+        *([vm(dsrc.shape, jnp.int32)] * 5),
         vm((rows, nf, ox, ln), F32), dma((rows,)), dma((rows,)),
         *pair(fo), *pair(ox), *pair(fa), *pair(ax), *pair(nf), *pair(ax),
         dma((6, 2)), dma((6, 2)),
         vm((rows, nf, ox, ln), F32), vm((rows, nf, ox, ln), F32), dma((rows,)), dma((rows,)),
-        vm((fa, ax, ln), F32), vm(atm.shape, F32), vm(oce.shape, F32), vm((nf, ax, ln), F32),
+        vm((fa, ax, ln), F32), vm((nf, ax, ln), F32),
         vm((ent, 2 * rows * nf * ox), BF16), vm((nf * ax, ent), BF16),
         vm((ent, 2 * nf * ax), BF16), vm((rows * nf * ox, ent), BF16),
-        vm((ent, ln), F32), vm((ent, ln), F32), dma((4,)),
+        vm((ent, ln), F32), vm((ent, ln), F32),
     ]
-    hbm = pl.BlockSpec(memory_space=pl.ANY)
+    args = (atm, oce, coup, dw, dsrc, drow, dblk, uw, udst, usrc)
+    args = [pltpu.with_memory_space_constraint(x, pltpu.HBM) for x in args]
+    hbm = pl.BlockSpec(memory_space=pltpu.HBM)
     small = pl.BlockSpec(memory_space=pltpu.VMEM)
-    return pl.pallas_call(
+    held = pl.pallas_call(
         functools.partial(kernel, sizes),
         out_shape=(
             jax.ShapeDtypeStruct(atm.shape, F32),
             jax.ShapeDtypeStruct(oce.shape, F32),
         ),
-        in_specs=[hbm, hbm, hbm, hbm, small, small, small, hbm, small, small],
+        in_specs=[hbm] * len(args),
+        out_specs=(small, small),
+        scratch_shapes=scratch,
+        compiler_params=pltpu.CompilerParams(collective_id=0, has_side_effects=True, vmem_limit_bytes=24 << 20
+        ),
+        name="coupled_step",
+    )(*args)
+    return pl.pallas_call(
+        write_out,
+        out_shape=(jax.ShapeDtypeStruct(atm.shape, F32), jax.ShapeDtypeStruct(oce.shape, F32)),
+        in_specs=[small, small],
         out_specs=(hbm, hbm),
-        scratch_shapes=scratch,
-        compiler_params=pltpu.CompilerParams(collective_id=0, has_side_effects=True),
-        name="coupled_step",
-    )(atm, oce, coup, dw, dsrc, drow, dblk, uw, udst, usrc)
+        scratch_shapes=[dma((2,))],
+        compiler_params=pltpu.CompilerParams(vmem_limit_bytes=8 << 20),
+        name="write_out",
+    )(*held)
 
 
 def solution(mesh):

time: 23.4 us -> 20.3 us (0.87)
  local copies, waits for them, and re-layouts: 2.42 us -> 0 us
  Pallas kernels: 20.2 us -> 19.5 us
    unnamed x4 -> x0, local copies, waits for them, and re-layouts: 2.42 us -> none
    pallas_call x1, Pallas kernels: 20.2 us -> 18.7 us  [body(): pl.pallas_call(functools.partial(kernel, sizes), out_shape=(jax.ShapeDtyp...]
    pallas_call x0 -> x1, Pallas kernels: none -> 0.81 us  [body(): pl.pallas_call(write_out, out_shape=(jax.ShapeDtypeStruct(atm.shape, F32)...]
where the time goes in v2:
time: 20.3 us; the launch traced here: 20.1 us
  Pallas kernels  19.5 us (96%)
  between operations  0.64 us (3%)
    pallas_call x1, Pallas kernels, body(): pl.pallas_call(functools.partial(kernel, sizes), out_shape=(jax.ShapeDtyp...  18.7 us
    pallas_call x1, Pallas kernels, body(): pl.pallas_call(write_out, out_shape=(jax.ShapeDtypeStruct(atm.shape, F32)...  0.81 us

profile of v2, /device:TPU:1, one launch (start us, length us, event | category | flops | bytes accessed | tf_op | source)
XLA Modules:
  0.0 20.1 jit_solution(15825625001618433352)
XLA Ops:
  0.6 18.7 %coupled_step.1 = (f32[4,4,32,128]{3,2,1,0:T(8,128)S(1)}, f32[4,8,16,128]{3,2,1,0:T(8,128)S(1)}) custom-call(f32[4,4,32,128]{3,2,1,0:T(8,128)} %atm.1, f32[4,8,16,128]{3,2,1,0:T(8,128)} %oce.1, f32[32,128]{1,0:T(8,128)} %coup.1, bf16[1,32,128,128]{3,2,1,0:T(8,128)(2,1)} %dw.1, s32[1,32]{1,0:T(1,128)} %dsrc_h.1, s32[1,32]{1,0:T(1,128)} %drow_h.1, ...), custom_call_target="tpu_custom_call" | custom-call | tf_op jit(solution)/shard_map/coupled_step/pallas_call | solution.py:365
  19.3 0.8 %write_out.1 = (f32[4,4,32,128]{3,2,1,0:T(8,128)}, f32[4,8,16,128]{3,2,1,0:T(8,128)}) custom-call(f32[4,4,32,128]{3,2,1,0:T(8,128)S(1)} %get-tuple-element.4.a, f32[4,8,16,128]{3,2,1,0:T(8,128)S(1)} %get-tuple-element.5.o), custom_call_target="tpu_custom_call" | custom-call | tf_op jit(solution)/shard_map/write_out/pallas_call | solution.py:378

commit v3 on v2

--- a/solution.py
+++ b/solution.py
@@ -61,7 +61,7 @@
     aov, oov,
     av, ov, cv, dwv, uwv, in_sem, usrc, udst, dsrc, drow, dblk,
     land, land_s, land_r,
-    oxs, oxr, oys, oyr, axs, axr, ays, ayr, fxs, fxr, fys, fyr, halo_s, halo_r,
+    oxs, oxr, oys, oyr, axs, axr, ays, ayr, fxs, fxr, fys, fyr, halo_s, halo_r, fx_s, fx_r, relay,
     dns, dnr, dn_s, dn_r,
     ub, flb, sel_u, t_u, sel_d, t_d, picked, rem,
 ):
@@ -98,10 +98,17 @@
     def y_neighbour(step):
         return {"cols": lax.rem(k + step + cols, cols)}
 
+    def corner(step, side):
+        return {**x_neighbour(step), **y_neighbour(side)}
+
     def row_peer(step):
         return {"rows": r ^ step}
 
-    partners = [x_neighbour(-1), x_neighbour(1), y_neighbour(-1), y_neighbour(1)]
+    def comp_neighbour(step):
+        return {"comp": lax.rem(c + step + comps, comps)}
+
+    across = [comp_neighbour(-1), comp_neighbour(1)] if comps > 1 else []
+    partners = [y_neighbour(-1), y_neighbour(1)] + across
     partners += [row_peer(d) for d in range(1, rows)]
     barrier = pltpu.get_barrier_semaphore()
     for who in partners:
@@ -143,7 +150,8 @@
     surface = [
         send(ov.at[:, 0], land.at[d], land_s.at[d], land_r.at[d], row_peer(d)) for d in order
     ]
-    sea_y = exchange(1, oys, oyr, y_neighbour)
+    for who in across:
+        pl.semaphore_signal(relay, inc=1, device_id=who, device_id_type=MESH)
     land[0] = ov[:, 0]
 
     second = gll_second() * VISCOSITY
@@ -177,6 +185,11 @@
                 if t == ax // 8 - 1:
                     axs[1, q : q + 1, :] = u[7:8, :]
 
+    if across:
+        pl.semaphore_wait(relay, len(across))
+    sea_y = exchange(1, oys, oyr, y_neighbour)
+    atm_x = exchange(2, axs, axr, x_neighbour)
+
     for copy in tables:
         copy.wait()
     def column(ref):
@@ -223,17 +236,28 @@
 
     ins[2].wait()
     ins[3].wait()
-    for copy in surface:
+    for copy in surface + sea_y:
         copy.wait_recv()
-    atm_x = exchange(2, axs, axr, x_neighbour)
     sea_x = exchange(0, oxs, oxr, x_neighbour)
     sea = remap(sel_u, land[...].reshape(rows * nf * ox, ln), uwv, t_u)
     flux = cv[...] * (sea.reshape(nf, ax, ln) - av[:, al - 1])
     flb[...] = flux
-    for f in range(nf):
-        fxs[0, f : f + 1, :] = flb[f, 0:1, :]
-        fxs[1, f : f + 1, :] = flb[f, ax - 1 : ax, :]
-    flux_x = exchange(4, fxs, fxr, x_neighbour)
+    west = jnp.zeros((ax, ln), F32)
+    east = jnp.zeros((ax, ln), F32)
+    for f in range(nf):
+        e = flux[f]
+        fxs[0, f : f + 1, :] = e[0:1, :]
+        fxs[1, f : f + 1, :] = e[ax - 1 : ax, :]
+        west = jnp.where(lane == f, e[:, 0:1], west)
+        east = jnp.where(lane == f, e[:, ln - 1 : ln], east)
+    fys[0] = west
+    fys[1] = east
+    flux_x = [
+        send(fxs.at[i], fxr.at[i, j], fx_s.at[i, j], fx_r.at[i, j], corner(step, side))
+        for i, step in enumerate((-1, 1))
+        for j, side in enumerate((-1, 0, 1))
+    ]
+    flux_y = exchange(4, fys, fyr, y_neighbour)
 
     ins[4].wait()
     down = remap(sel_d, flb[...].reshape(nf * ax, ln), dwv, t_d)
@@ -272,7 +296,7 @@
     x_pass(atm_x, axr, ub, ays, nf * al)
     atm_y = exchange(3, ays, ayr, y_neighbour)
 
-    for copy in sea_x + sea_y:
+    for copy in sea_x:
         copy.wait_recv()
     o_row = iota((ox, ln), 0)
     o_lane = iota((ox, ln), 1)
@@ -294,9 +318,6 @@
         for l in range(ol):
             stencil(f, l)
 
-    x_pass(flux_x, fxr, flb, fys, nf)
-    flux_y = exchange(5, fys, fyr, y_neighbour)
-
     for copy in atm_y:
         copy.wait_recv()
     before, after = ayr[1], ayr[0]
@@ -305,11 +326,20 @@
             q = f * al + l
             aov[f, l] = average(ub[q], 1, before[:, q : q + 1], after[:, q : q + 1])
 
-    for copy in flux_y:
+    for copy in flux_x + flux_y:
         copy.wait_recv()
-    before, after = fyr[1], fyr[0]
-    for f in range(nf):
-        e = average(flb[f], 1, before[:, f : f + 1], after[:, f : f + 1])
+
+    def corners(i, j, at):
+        row = jnp.zeros((1, ln), F32)
+        for f in range(nf):
+            row = jnp.where(lane == f, fxr[i, j, f : f + 1, at : at + 1], row)
+        return row
+
+    before = average(fyr[1], 0, corners(1, 2, ln - 1), corners(0, 2, ln - 1))
+    after = average(fyr[0], 0, corners(1, 0, 0), corners(0, 0, 0))
+    for f in range(nf):
+        e = average(flb[f], 0, fxr[1, 1, f : f + 1, :], fxr[0, 1, f : f + 1, :])
+        e = average(e, 1, before[:, f : f + 1], after[:, f : f + 1])
         aov[f, al - 1] = aov[f, al - 1] + ATM_GAIN * e
 
     for copy in going:
@@ -350,8 +380,10 @@
         vm((nb, blk, blk), BF16), vm((nb, blk, blk), BF16), dma((10,)),
         *([vm(dsrc.shape, jnp.int32)] * 5),
         vm((rows, nf, ox, ln), F32), dma((rows,)), dma((rows,)),
-        *pair(fo), *pair(ox), *pair(fa), *pair(ax), *pair(nf), *pair(ax),
-        dma((6, 2)), dma((6, 2)),
+        *pair(fo), *pair(ox), *pair(fa), *pair(ax),
+        vm((2, nf, ln), F32), vm((2, 3, nf, ln), F32), *pair(ax),
+        dma((5, 2)), dma((5, 2)), dma((2, 3)), dma((2, 3)),
+        pltpu.SemaphoreType.REGULAR,
         vm((rows, nf, ox, ln), F32), vm((rows, nf, ox, ln), F32), dma((rows,)), dma((rows,)),
         vm((fa, ax, ln), F32), vm((nf, ax, ln), F32),
         vm((ent, 2 * rows * nf * ox), BF16), vm((nf * ax, ent), BF16),

time: 20.3 us -> 18.6 us (0.916)
  the two profiles are of different devices: /device:TPU:1 before, /device:TPU:0 now
where the time goes in v3:
time: 18.6 us; the launch traced here: 18.5 us
  Pallas kernels  17.8 us (96%)
  between operations  0.64 us (3%)
    pallas_call x1, Pallas kernels, body(): pl.pallas_call(functools.partial(kernel, sizes), out_shape=(jax.ShapeDtyp...  17 us
    pallas_call x1, Pallas kernels, body(): pl.pallas_call(write_out, out_shape=(jax.ShapeDtypeStruct(atm.shape, F32)...  0.81 us

profile of v3, /device:TPU:0, one launch (start us, length us, event | category | flops | bytes accessed | tf_op | source)
XLA Modules:
  0.0 18.5 jit_solution(13569403512141542184)
XLA Ops:
  0.6 17.0 %coupled_step.1 = (f32[4,4,32,128]{3,2,1,0:T(8,128)S(1)}, f32[4,8,16,128]{3,2,1,0:T(8,128)S(1)}) custom-call(f32[4,4,32,128]{3,2,1,0:T(8,128)} %atm.1, f32[4,8,16,128]{3,2,1,0:T(8,128)} %oce.1, f32[32,128]{1,0:T(8,128)} %coup.1, bf16[1,32,128,128]{3,2,1,0:T(8,128)(2,1)} %dw.1, s32[1,32]{1,0:T(1,128)} %dsrc_h.1, s32[1,32]{1,0:T(1,128)} %drow_h.1, ...), custom_call_target="tpu_custom_call" | custom-call | tf_op jit(solution)/shard_map/coupled_step/pallas_call | solution.py:397
  17.7 0.8 %write_out.1 = (f32[4,4,32,128]{3,2,1,0:T(8,128)}, f32[4,8,16,128]{3,2,1,0:T(8,128)}) custom-call(f32[4,4,32,128]{3,2,1,0:T(8,128)S(1)} %get-tuple-element.4.a, f32[4,8,16,128]{3,2,1,0:T(8,128)S(1)} %get-tuple-element.5.o), custom_call_target="tpu_custom_call" | custom-call | tf_op jit(solution)/shard_map/write_out/pallas_call | solution.py:410
